TPU v7x, 256 devices: a whole 4x4x8 slice. The times are simulated.
256 devices in a mesh: items: 4 (over x), users: 64 (over z, y, core).
Axes of the slice: x: 4, y: 4, z: 8, core: 2. Of those that a mesh axis runs over, the one named last changes fastest.
Arguments:
- capsules: bfloat16 [4096, 8, 128], P('users'), may hold values from -6 to 6
- bank: bfloat16 [262144, 128], P(('items', 'users')), may hold values from -0.5 to 0.5
Outputs:
- relative: float32 [4096, 256], P('users', 'items')
- peak: float32 [4096], P('users')
All inputs are finite; a program needn't handle non-finite values.
Results may differ from a plain program's by a relative error of at most 0.0003.
Values may be sent and summed in bfloat16 or wider, within the bound.
No kernel may reach another device: no remote copies, remote signals or barrier semaphores. Data moves between devices by JAX's collectives and lax.ppermute only.
A program may use at most 64 MiB of HBM per device.

v0:
```python
import jax
import jax.numpy as jnp
from jax import lax
from jax.sharding import PartitionSpec as P

BLOCK = 1024


def sent_to_all(value, axis):
    length = lax.axis_size(axis)
    return lax.all_to_all(
        jnp.broadcast_to(value[None], (length, *value.shape)), axis, 0, 0, tiled=True
    )


def of_everyone(value, axis):
    return sent_to_all(value, axis).max(axis=0)


def block_peaks(caps, rows):
    users_here = caps.shape[0]
    flat = caps.reshape(users_here * caps.shape[1], caps.shape[2])
    count = rows.shape[0] // BLOCK
    blocks = rows.reshape(count, BLOCK, rows.shape[1])

    def one_block(item_rows):
        score = lax.dot_general(
            flat, item_rows, (((1,), (1,)), ((), ())), preferred_element_type=jnp.float32
        )
        return jnp.max(score.reshape(users_here, -1), axis=1)

    return lax.map(one_block, blocks).T


def per_device(capsules, bank):
    everyone = lax.all_gather(capsules, "users", axis=0, tiled=True)
    own_block = block_peaks(everyone, bank)
    table = lax.all_to_all(own_block, "users", split_axis=0, concat_axis=1, tiled=True)
    peak = of_everyone(jnp.max(table, axis=1), "items")
    return (table - peak[:, None], peak)


def solution(mesh):
    return jax.shard_map(
        per_device,
        mesh=mesh,
        in_specs=(P("users", None, None), P(("items", "users"), None)),
        out_specs=(P("users", "items"), P("users")),
        check_vma=False,
    )
```

profile of v0, /device:TPU:1, one launch (start us, length us, event | category | flops | bytes accessed | tf_op | source)
XLA Modules:
  0.0 152.0 jit_solution(13896020500113062206)
XLA Ops:
  7.2 0.0 copy-start
  7.2 0.0 all-gather.2.cloned.1.call-start
  7.2 0.7 all-gather.2.cloned.1.call-update
  7.9 90.1 %all-gather.2.cloned.1.call-done = bf16[4096,8,128]{2,1,0:T(8,128)(2,1)} async-done(((bf16[64,8,128]{2,1,0:T(8,128)(2,1)}), bf16[4096,8,128]{2,1,0:T(8,128)(2,1)}) %all-gather.2.cloned.1.call-update) | async-done | bytes 8388624 | tf_op jit(solution)/shard_map/all_gather | solution.py:36
  98.0 0.0 copy-done
  98.0 21.6 %convolution_reduce_fusion = f32[32768]{0:T(1024)S(1)} fusion(bf16[1024,128]{1,0:T(8,128)(2,1)S(1)} %copy-done, bf16[4096,8,128]{2,1,0:T(8,128)(2,1)} %all-gather.2.cloned.1.call-done), kind=kOutput, calls=%fused_computation | convolution fusion | flops 8623456256 | bytes 8781824 | tf_op jit(solution)/shard_map/while/body/eval_jaxpr/dot_general | solution.py:27
  119.6 1.1 reduce_max.36
  120.7 0.6 reduce_max.37
  121.3 0.1 all_to_all.18
  121.4 15.0 %all_to_all.25 = f32[64,64,1]{1,2,0:T(1,128)S(1)} all-to-all(f32[64,64,1]{1,2,0:T(1,128)S(1)} %bitcast.10), channel_id=1, replica_groups=mesh['items'=4,'users'=64] {'users'}, dimensions={0} | all-to-all | bytes 32768 | tf_op jit(solution)/shard_map/all_to_all | solution.py:38
  136.4 0.1 reduce_max.38
  136.5 7.9 %all_to_all.26 = f32[4,1,64]{2,1,0:T(1,128)S(1)} all-to-all(f32[4,1,64]{2,1,0:T(1,128)S(1)} %broadcast_in_dim.5), channel_id=1, replica_groups=mesh['items'=4,'users'=64] {'items'}, dimensions={0} | all-to-all | bytes 2048 | tf_op jit(solution)/shard_map/all_to_all | solution.py:11
  144.4 0.0 copy-start.1
  144.4 0.7 copy.11
  145.1 0.0 copy-done.1
  (3 shorter events, 0.0 us)
Async XLA Ops:
  7.2 90.8 %copy-start = (bf16[1024,128]{1,0:T(8,128)(2,1)S(1)}, bf16[1024,128]{1,0:T(8,128)(2,1)}, u32[]{:S(2)}) copy-start(bf16[1024,128]{1,0:T(8,128)(2,1)} %param.3) | copy-start | bytes 786436
  7.2 90.8 %all-gather.2.cloned.1.call-start = ((), (), s32[]{:S(2)}) async-start(), calls=%async_computation.2 | async-start | bytes 8519680 | tf_op jit(solution)/shard_map/all_gather | solution.py:36
  144.4 0.7 copy-start.1
Sparse Core Ops, SparseCore 0:
  10.8 87.1 all-gather.1
where the time goes:
time: 152 us
  waiting for transfers between devices  90.8 us (60%)
  blocking collectives  22.9 us (15%)
  matrix products  21.6 us (14%)
  between operations  14.1 us (9%)
  local copies, waits for them, and re-layouts  1.92 us (1%)
    all_gather x1, waiting for transfers between devices, per_device(): everyone = lax.all_gather(capsules, 'users', axis=0, tiled=True)  90.1 us
    dot_general x1, matrix products, one_block(): lax.dot_general(flat, item_rows, (((1,), (1,)), ((), ())), preferred_elem...  21.6 us
    all_to_all x1, blocking collectives, per_device(): lax.all_to_all(own_block, 'users', split_axis=0, concat_axis=1, tiled=True)  15 us
    all_to_all x1, blocking collectives, sent_to_all(): lax.all_to_all(jnp.broadcast_to(value[None], (length, *value.shape)), axi...  7.9 us
  transfers between devices with their start and end apart: 1, of which 1 were waited for; matrix products, arithmetic and copies ran while one was open for 0% of the time, Pallas kernels for 0%

commit v1 on v0

v1 whole, which is shorter than its diff:
```python
import jax
import jax.numpy as jnp
from jax import lax
from jax.experimental import pallas as pl
from jax.experimental.pallas import tpu as pltpu
from jax.sharding import Mesh, PartitionSpec as P

BLOCK = 1024
AXES = ("x", "z", "y", "c")
SIZES = (4, 8, 4, 2)
NEG = float("-inf")
LIMIT = 16 << 20
VMEM = pl.BlockSpec(memory_space=pltpu.VMEM)


def flat(x, z, y, c):
    return ((x * SIZES[1] + z) * SIZES[2] + y) * SIZES[3] + c


def move(value, target):
    pairs = []
    for x in range(SIZES[0]):
        for z in range(SIZES[1]):
            for y in range(SIZES[2]):
                for c in range(SIZES[3]):
                    pairs.append((flat(x, z, y, c), flat(*target(x, z, y, c))))
    return lax.ppermute(value, AXES, pairs)


def along(c):
    return 2 * c - 1


def to_partner(value):
    return move(value, lambda x, z, y, c: (x, z, y, 1 - c))


def down_z(value):
    return move(value, lambda x, z, y, c: (x, (z - along(c)) % SIZES[1], y, c))


def down_y(value):
    return move(value, lambda x, z, y, c: (x, z, (y - along(c)) % SIZES[2], c))


def score_rows(caps, items):
    flat_caps = caps
    best = None
    for at in range(0, BLOCK, 256):
        score = lax.dot_general(
            items[at : at + 256], flat_caps, (((1,), (1,)), ((), ())),
            preferred_element_type=jnp.float32,
        )
        part = jnp.max(score.reshape(32, 8, 512), axis=0)
        best = part if best is None else jnp.maximum(best, part)
    return jnp.max(best, axis=0, keepdims=True)


def pieces(refs, height):
    return [(r, at) for r in refs for at in range(0, r.shape[0], height)]


def scores(groups, blocks):
    n_groups, n_blocks = len(groups), len(blocks)

    def body(*refs):
        out = refs[-1]
        caps = pieces(refs[:n_groups], 512)
        items = pieces(refs[n_groups:-1], BLOCK)
        for g, (cref, cat) in enumerate(caps):
            own = cref[cat : cat + 512, :]
            for b, (iref, iat) in enumerate(items):
                out[pl.ds(g * len(items) + b, 1), :] = score_rows(own, iref.at[iat : iat + BLOCK, :])

    rows = sum(v.shape[0] // 512 for v in groups) * sum(v.shape[0] // BLOCK for v in blocks)
    return pl.pallas_call(
        body,
        out_shape=jax.ShapeDtypeStruct((rows, 512), jnp.float32),
        in_specs=[VMEM] * (n_groups + n_blocks),
        out_specs=VMEM,
        compiler_params=pltpu.CompilerParams(vmem_limit_bytes=LIMIT),
        cost_estimate=pl.CostEstimate(
            flops=rows * 2 * 512 * BLOCK * 128 * 2, bytes_accessed=1 << 16, transcendentals=0
        ),
    )(*groups, *blocks)


def gather_rows(parts, places):
    def body(*refs):
        out, rows = refs[-2], refs[-1]
        z = lax.axis_index("z")
        y = lax.axis_index("y")
        c = lax.axis_index("c")
        step = 2 * c - 1
        for ref, place in zip(refs, places):
            for r, (group, (dy, other)) in enumerate(place):
                at_y = (y + step * dy + 4) % 4
                at_c = 1 - c if other else c
                rows[pl.ds(group * 8 + at_y * 2 + at_c, 1), :] = ref[r : r + 1, :]
        by_capsule = rows[...].T
        by_user = jnp.max(by_capsule.reshape(64, 8, 64), axis=1)
        peaks = jnp.concatenate([by_user, jnp.zeros((64, 64), jnp.float32)], axis=0).T
        out[...] = jnp.full(out.shape, NEG, jnp.float32)
        for group, (dz, other) in enumerate(GROUPS):
            at_z = (z + step * dz + 8) % 8
            at_c = 1 - c if other else c
            for x in range(4):
                out[x * 16 + at_z * 2 + at_c] = peaks[group * 8 : group * 8 + 8, :]

    return pl.pallas_call(
        body,
        out_shape=jax.ShapeDtypeStruct((64, 8, 128), jnp.float32),
        in_specs=[VMEM] * len(parts),
        out_specs=VMEM,
        compiler_params=pltpu.CompilerParams(vmem_limit_bytes=LIMIT),
        scratch_shapes=[pltpu.VMEM((64, 512), jnp.float32)],
    )(*parts)


GROUPS = [(0, 0), (1, 0), (1, 1), (2, 0), (2, 1), (3, 0), (3, 1), (4, 0)]


def finish(table):
    def body(table_ref, relative, peak):
        x = lax.axis_index("x")
        best = jnp.max(table_ref[...], axis=0)
        top = jnp.max(best, axis=0, keepdims=True)
        mine = jnp.concatenate(
            [jnp.maximum(table_ref[x * 16 + 2 * z], table_ref[x * 16 + 2 * z + 1]) for z in range(8)], axis=0
        )
        relative[...] = (mine - top).T[:64, :]
        peak[...] = top[0, :64]

    return pl.pallas_call(
        body,
        out_shape=(jax.ShapeDtypeStruct((64, 64), jnp.float32), jax.ShapeDtypeStruct((64,), jnp.float32)),
        in_specs=[VMEM],
        compiler_params=pltpu.CompilerParams(vmem_limit_bytes=LIMIT),
        out_specs=(VMEM, VMEM),
    )(table)


def per_device(capsules, bank):
    own = capsules.reshape(512, 128)
    own_pair = jnp.concatenate([own, to_partner(own)], axis=0)
    block_pair = jnp.concatenate([bank, to_partner(bank)], axis=0)
    z1 = down_z(own_pair)
    z2 = down_z(z1)
    z3 = down_z(z2)
    z4 = down_z(z3[:512])
    y1 = down_y(block_pair)
    y2 = down_y(y1[:BLOCK])
    y1x = to_partner(y1)
    y2x = to_partner(y2)
    b0 = [(0, 0), (0, 1)]
    b1 = [(1, 0), (1, 1)]
    b1x = [(-1, 1), (-1, 0)]
    b2 = [(2, 0)]
    b2x = [(2, 1)]

    plan = [
        ([own], [0], [block_pair], b0),
        ([z1], [1, 2], [block_pair], b0),
        ([own, z1], [0, 1, 2], [y1], b1),
        ([own, z1], [0, 1, 2], [y1x], b1x),
        ([z2], [3, 4], [block_pair, y1, y1x], b0 + b1 + b1x),
        ([own, z1, z2], [0, 1, 2, 3, 4], [y2, y2x], b2 + b2x),
        ([z3], [5, 6], [block_pair, y1, y1x, y2, y2x], b0 + b1 + b1x + b2 + b2x),
        ([z4], [7], [block_pair, y1, y1x, y2, y2x], b0 + b1 + b1x + b2 + b2x),
    ]
    parts, places = [], []
    for groups, ids, blocks, names in plan:
        parts.append(scores(groups, blocks))
        places.append([(g, b) for g in ids for b in names])
    ready = gather_rows(parts, places)
    table = lax.all_to_all(ready, ("x", "z", "c"), 0, 0, tiled=True)
    return finish(table)


def solution(mesh):
    grid = Mesh(mesh.devices.reshape(SIZES), AXES)
    return jax.shard_map(
        per_device,
        mesh=grid,
        in_specs=(P(("z", "y", "c"), None, None), P(AXES, None)),
        out_specs=(P(("z", "y", "c"), "x"), P(("z", "y", "c"))),
        check_vma=False,
    )
```

time: 152 us -> 69.2 us (0.46)
  waiting for transfers between devices: 90.8 us -> 6.94 us
  matrix products: 21.6 us -> 0 us
  Pallas kernels: 0 us -> 20.2 us
  starting transfers between devices: 0.04 us -> 19.6 us
  between operations: 14.1 us -> 0.75 us
  blocking collectives: 22.9 us -> 20.4 us
    all_gather x1 -> x0, waiting for transfers between devices: 90.1 us -> none  [per_device(): everyone = lax.all_gather(capsules, 'users', axis=0, tiled=True)]
    dot_general x1 -> x0, matrix products: 21.6 us -> none  [one_block(): lax.dot_general(flat, item_rows, (((1,), (1,)), ((), ())), preferred_elem...]
    pallas_call x0 -> x10, Pallas kernels: none -> 20.2 us  [the longest x8 19.1 us: scores(): pl.pallas_call(body, out_shape=jax.ShapeDtypeStruct((rows, 512), jnp.floa...]
    ppermute x0 -> x10, starting transfers between devices: none -> 19.6 us  [move(): return lax.ppermute(value, AXES, pairs)]
    ppermute x0 -> x10, waiting for transfers between devices: none -> 6.94 us  [move(): return lax.ppermute(value, AXES, pairs)]
    all_to_all x2 -> x1, blocking collectives: 22.9 us -> 20.4 us  [per_device(): table = lax.all_to_all(ready, ('x', 'z', 'c'), 0, 0, tiled=True)]
  transfers between devices with their start and end apart: 1 -> 10, of which waited for: 1 -> 3; matrix products, arithmetic and copies ran while one was open for 0% -> 2% of each run, Pallas kernels for 0% -> 24%
where the time goes in v1:
time: 69.2 us; the launch traced here: 69 us
  blocking collectives  20.4 us (29%)
  Pallas kernels  20.2 us (29%)
  starting transfers between devices  19.6 us (28%)
  waiting for transfers between devices  6.94 us (10%)
  local copies, waits for them, and re-layouts  1.04 us (2%)
  between operations  0.75 us (1%)
    all_to_all x1, blocking collectives, per_device(): table = lax.all_to_all(ready, ('x', 'z', 'c'), 0, 0, tiled=True)  20.4 us
    ppermute x10, starting transfers between devices, move(): return lax.ppermute(value, AXES, pairs)  19.6 us
    pallas_call x8, Pallas kernels, scores(): pl.pallas_call(body, out_shape=jax.ShapeDtypeStruct((rows, 512), jnp.floa...  19.1 us
    ppermute x10, waiting for transfers between devices, move(): return lax.ppermute(value, AXES, pairs)  6.94 us
  transfers between devices with their start and end apart: 10, of which 3 were waited for; matrix products, arithmetic and copies ran while one was open for 2% of the time, Pallas kernels for 24%

profile of v1, /device:TPU:1, one launch (start us, length us, event | category | flops | bytes accessed | tf_op | source)
XLA Modules:
  0.0 69.0 jit_solution(7359370257999196718)
XLA Ops:
  0.6 3.3 %collective-permute-start = (bf16[1024,128]{1,0:T(8,128)(2,1)}, bf16[1024,128]{1,0:T(8,128)(2,1)S(1)}, u32[]{:S(2)}, u32[]{:S(2)}) collective-permute-start(bf16[1024,128]{1,0:T(8,128)(2,1)} %param.3), channel_id=1, source_target_pairs={{0,1},{1,0},{2,3},{3,2},{4,5},{5,4},{6,7},{7,6},{8,9},{9,8},{10,11... | collective-permute-start | bytes 786440 | tf_op jit(solution)/shard_map/ppermute | solution.py:27
  3.9 0.1 collective-permute-start.1
  4.0 1.0 %constant_dynamic-update-slice_fusion.1 = bf16[2048,128]{1,0:T(8,128)(2,1)S(1)} fusion(bf16[1024,128]{1,0:T(8,128)(2,1)} %param.3), kind=kLoop, calls=%fused_computation.2 | loop fusion | bytes 524288
  5.0 0.0 copy-start
  5.0 0.3 collective-permute-done
  5.3 1.1 %collective-permute-start.3 = (bf16[2048,128]{1,0:T(8,128)(2,1)S(1)}, bf16[2048,128]{1,0:T(8,128)(2,1)S(1)}, u32[]{:S(2)}, u32[]{:S(2)}) collective-permute-start(bf16[2048,128]{1,0:T(8,128)(2,1)S(1)} %constant_dynamic-update-slice_fusion.refs_1_), channel_id=1, source_target_pairs={{0,2},{1,7},{2,4},{3,1},{4,6},{5,3},{6,0},{7,5},{8,10},{9,15},{10,... | collective-permute-start | bytes 1572872 | tf_op jit(solution)/shard_map/ppermute | solution.py:27
  6.4 0.0 collective-permute-done.1
  6.5 5.7 %collective-permute-start.2 = (bf16[1024,128]{1,0:T(8,128)(2,1)S(1)}, bf16[1024,128]{1,0:T(8,128)(2,1)S(1)}, u32[]{:S(2)}, u32[]{:S(2)}) collective-permute-start(bf16[1024,128]{1,0:T(8,128)(2,1)S(1)} %pad_maximum_fusion), channel_id=1, source_target_pairs={{0,8},{1,57},{2,10},{3,59},{4,12},{5,61},{6,14},{7,63},{8,16},{9,1... | collective-permute-start | bytes 786440 | tf_op jit(solution)/shard_map/ppermute | solution.py:27
  12.1 3.3 %collective-permute-done.2.refs_0_.refs_1_ = bf16[1024,128]{1,0:T(8,128)(2,1)S(1)} collective-permute-done((bf16[1024,128]{1,0:T(8,128)(2,1)S(1)}, bf16[1024,128]{1,0:T(8,128)(2,1)S(1)}, u32[]{:S(2)}, u32[]{:S(2)}) %collective-permute-start.2) | collective-permute-done | bytes 262176 | tf_op jit(solution)/shard_map/ppermute | solution.py:27
  15.4 3.4 %collective-permute-start.5 = (bf16[1024,128]{1,0:T(8,128)(2,1)S(1)}, bf16[1024,128]{1,0:T(8,128)(2,1)S(1)}, u32[]{:S(2)}, u32[]{:S(2)}) collective-permute-start(bf16[1024,128]{1,0:T(8,128)(2,1)S(1)} %collective-permute-done.2.refs_0_.refs_1_), channel_id=1, source_target_pairs={{0,8},{1,57},{2,10},{3,59},{4,12},{5,61},{6,14},{7,63},{8,16},{9,1... | collective-permute-start | bytes 786440 | tf_op jit(solution)/shard_map/ppermute | solution.py:27
  18.8 0.0 collective-permute-done.3.refs_2_
  18.8 0.0 collective-permute-start.4
  18.8 3.3 %collective-permute-done.5.refs_0_.refs_2_ = bf16[1024,128]{1,0:T(8,128)(2,1)S(1)} collective-permute-done((bf16[1024,128]{1,0:T(8,128)(2,1)S(1)}, bf16[1024,128]{1,0:T(8,128)(2,1)S(1)}, u32[]{:S(2)}, u32[]{:S(2)}) %collective-permute-start.5) | collective-permute-done | bytes 262176 | tf_op jit(solution)/shard_map/ppermute | solution.py:27
  22.2 3.1 %collective-permute-start.8 = (bf16[1024,128]{1,0:T(8,128)(2,1)S(1)}, bf16[1024,128]{1,0:T(8,128)(2,1)S(1)}, u32[]{:S(2)}, u32[]{:S(2)}) collective-permute-start(bf16[1024,128]{1,0:T(8,128)(2,1)S(1)} %collective-permute-done.5.refs_0_.refs_2_), channel_id=1, source_target_pairs={{0,8},{1,57},{2,10},{3,59},{4,12},{5,61},{6,14},{7,63},{8,16},{9,1... | collective-permute-start | bytes 786440 | tf_op jit(solution)/shard_map/ppermute | solution.py:27
  25.3 0.3 collective-permute-start.6
  25.6 0.7 %shard_map.41.refs_0_ = f32[2,512]{1,0:T(2,128)S(1)} custom-call(bf16[512,128]{1,0:T(8,128)(2,1)S(1)} %bitcast.3, bf16[2048,128]{1,0:T(8,128)(2,1)S(1)} %constant_dynamic-update-slice_fusion.refs_1_), custom_call_target="tpu_custom_call" | custom-call | flops 536870912 | bytes 65536 | tf_op jit(solution)/shard_map/pallas_call | solution.py:76
  26.3 1.3 %shard_map.42.refs_1_ = f32[4,512]{1,0:T(4,128)S(1)} custom-call(bf16[1024,128]{1,0:T(8,128)(2,1)S(1)} %collective-permute-done.2.refs_0_.refs_1_, bf16[2048,128]{1,0:T(8,128)(2,1)S(1)} %constant_dynamic-update-slice_fusion.refs_1_), custom_call_target="tpu_custom_call" | custom-call | flops 1073741824 | bytes 65536 | tf_op jit(solution)/shard_map/pallas_call | solution.py:76
  27.6 1.8 %shard_map.43.refs_2_ = f32[6,512]{1,0:T(8,128)S(1)} custom-call(bf16[512,128]{1,0:T(8,128)(2,1)S(1)} %bitcast.4, bf16[1024,128]{1,0:T(8,128)(2,1)S(1)} %collective-permute-done.2.refs_0_.refs_1_, bf16[2048,128]{1,0:T(8,128)(2,1)S(1)} %collective-permute-done.3.refs_2_), custom_call_target="tpu_custom_call" | custom-call | flops 1610612736 | bytes 65536 | tf_op jit(solution)/shard_map/pallas_call | solution.py:76
  29.4 0.0 collective-permute-done.8.refs_0_
  29.4 2.7 %collective-permute-start.9 = (bf16[512,128]{1,0:T(8,128)(2,1)S(1)}, bf16[512,128]{1,0:T(8,128)(2,1)S(1)}, u32[]{:S(2)}, u32[]{:S(2)}) collective-permute-start(bf16[512,128]{1,0:T(8,128)(2,1)S(1)} %slice.9), channel_id=1, source_target_pairs={{0,8},{1,57},{2,10},{3,59},{4,12},{5,61},{6,14},{7,63},{8,16},{9,1... | collective-permute-start | bytes 393224 | tf_op jit(solution)/shard_map/ppermute | solution.py:27
  32.1 0.0 collective-permute-done.6.refs_3_.refs_4_
  32.1 0.0 collective-permute-start.7
  32.1 0.0 collective-permute-done.4.refs_2_.refs_3_
  32.1 3.5 %shard_map.45.refs_4_ = f32[12,512]{1,0:T(8,128)S(1)} custom-call(bf16[1024,128]{1,0:T(8,128)(2,1)S(1)} %collective-permute-done.5.refs_0_.refs_2_, bf16[2048,128]{1,0:T(8,128)(2,1)S(1)} %constant_dynamic-update-slice_fusion.refs_1_, bf16[2048,128]{1,0:T(8,128)(2,1)S(1)} %collective-permute-done.3.refs_2_, ...), custom_call_target="tpu_custom_call" | custom-call | flops 3221225472 | bytes 65536 | tf_op jit(solution)/shard_map/pallas_call | solution.py:76
  35.6 2.9 %shard_map.46.refs_5_ = f32[10,512]{1,0:T(8,128)S(1)} custom-call(bf16[512,128]{1,0:T(8,128)(2,1)S(1)} %bitcast.5, bf16[1024,128]{1,0:T(8,128)(2,1)S(1)} %collective-permute-done.2.refs_0_.refs_1_, bf16[1024,128]{1,0:T(8,128)(2,1)S(1)} %collective-permute-done.5.refs_0_.refs_2_, bf16[1024,128]{1,0:T(8,128)(2,1)S(1)} %collective-permute-done.6.refs_3_.refs_4_, ...), custom_call_target="tpu_custom_call" | custom-call | flops 2684354560 | bytes 65536 | tf_op jit(solution)/shard_map/pallas_call | solution.py:76
  38.5 4.5 %shard_map.47.refs_6_ = f32[16,512]{1,0:T(8,128)S(1)} custom-call(bf16[1024,128]{1,0:T(8,128)(2,1)S(1)} %collective-permute-done.8.refs_0_, bf16[2048,128]{1,0:T(8,128)(2,1)S(1)} %constant_dynamic-update-slice_fusion.refs_1_, bf16[2048,128]{1,0:T(8,128)(2,1)S(1)} %collective-permute-done.3.refs_2_, ...), custom_call_target="tpu_custom_call" | custom-call | flops 4294967296 | bytes 65536 | tf_op jit(solution)/shard_map/pallas_call | solution.py:76
  43.0 2.1 %shard_map.44.refs_3_ = f32[6,512]{1,0:T(8,128)S(1)} custom-call(bf16[512,128]{1,0:T(8,128)(2,1)S(1)} %bitcast.6, bf16[1024,128]{1,0:T(8,128)(2,1)S(1)} %collective-permute-done.2.refs_0_.refs_1_, bf16[2048,128]{1,0:T(8,128)(2,1)S(1)} %collective-permute-done.4.refs_2_.refs_3_), custom_call_target="tpu_custom_call" | custom-call | flops 1610612736 | bytes 65536 | tf_op jit(solution)/shard_map/pallas_call | solution.py:76
  45.1 0.0 collective-permute-done.9.refs_0_
  45.1 2.4 %shard_map.48.refs_7_ = f32[8,512]{1,0:T(8,128)S(1)} custom-call(bf16[512,128]{1,0:T(8,128)(2,1)S(1)} %collective-permute-done.9.refs_0_, bf16[2048,128]{1,0:T(8,128)(2,1)S(1)} %constant_dynamic-update-slice_fusion.refs_1_, bf16[2048,128]{1,0:T(8,128)(2,1)S(1)} %collective-permute-done.3.refs_2_, ...), custom_call_target="tpu_custom_call" | custom-call | flops 2147483648 | bytes 65536 | tf_op jit(solution)/shard_map/pallas_call | solution.py:76
  47.5 0.3 shard_map.49
  47.8 20.4 %all_to_all.5.table_ref = f32[64,8,128]{2,1,0:T(8,128)S(1)} all-to-all(f32[64,8,128]{2,1,0:T(8,128)S(1)} %shard_map.49), channel_id=1, replica_groups=mesh['x'=4,'z'=8,'y'=4,'c'=2] {'x','z','c'}, dimensions={0} | all-to-all | bytes 524288 | tf_op jit(solution)/shard_map/all_to_all | solution.py:176
  68.3 0.7 %shard_map.50 = (f32[64,64]{1,0:T(8,128)}, f32[64]{0:T(128)}) custom-call(f32[64,8,128]{2,1,0:T(8,128)S(1)} %all_to_all.5.table_ref), custom_call_target="tpu_custom_call" | custom-call | tf_op jit(solution)/shard_map/pallas_call | solution.py:134
  (6 shorter events, 0.1 us)
Async XLA Ops:
  0.6 4.7 %collective-permute-start = (bf16[1024,128]{1,0:T(8,128)(2,1)}, bf16[1024,128]{1,0:T(8,128)(2,1)S(1)}, u32[]{:S(2)}, u32[]{:S(2)}) collective-permute-start(bf16[1024,128]{1,0:T(8,128)(2,1)} %param.3), channel_id=1, source_target_pairs={{0,1},{1,0},{2,3},{3,2},{4,5},{5,4},{6,7},{7,6},{8,9},{9,8},{10,11... | collective-permute-start | bytes 786440 | tf_op jit(solution)/shard_map/ppermute | solution.py:27
  3.9 2.5 %collective-permute-start.1 = (bf16[512,128]{1,0:T(8,128)(2,1)}, bf16[512,128]{1,0:T(8,128)(2,1)S(1)}, u32[]{:S(2)}, u32[]{:S(2)}) collective-permute-start(bf16[512,128]{1,0:T(8,128)(2,1)} %bitcast.1), channel_id=1, source_target_pairs={{0,1},{1,0},{2,3},{3,2},{4,5},{5,4},{6,7},{7,6},{8,9},{9,8},{10,11... | collective-permute-start | bytes 393224 | tf_op jit(solution)/shard_map/ppermute | solution.py:27
  5.0 1.5 %copy-start = (bf16[64,8,128]{2,1,0:T(8,128)(2,1)S(1)}, bf16[64,8,128]{2,1,0:T(8,128)(2,1)}, u32[]{:S(2)}) copy-start(bf16[64,8,128]{2,1,0:T(8,128)(2,1)} %param.2) | copy-start | bytes 393220
  5.3 13.5 %collective-permute-start.3 = (bf16[2048,128]{1,0:T(8,128)(2,1)S(1)}, bf16[2048,128]{1,0:T(8,128)(2,1)S(1)}, u32[]{:S(2)}, u32[]{:S(2)}) collective-permute-start(bf16[2048,128]{1,0:T(8,128)(2,1)S(1)} %constant_dynamic-update-slice_fusion.refs_1_), channel_id=1, source_target_pairs={{0,2},{1,7},{2,4},{3,1},{4,6},{5,3},{6,0},{7,5},{8,10},{9,15},{10,... | collective-permute-start | bytes 1572872 | tf_op jit(solution)/shard_map/ppermute | solution.py:27
  6.5 9.0 %collective-permute-start.2 = (bf16[1024,128]{1,0:T(8,128)(2,1)S(1)}, bf16[1024,128]{1,0:T(8,128)(2,1)S(1)}, u32[]{:S(2)}, u32[]{:S(2)}) collective-permute-start(bf16[1024,128]{1,0:T(8,128)(2,1)S(1)} %pad_maximum_fusion), channel_id=1, source_target_pairs={{0,8},{1,57},{2,10},{3,59},{4,12},{5,61},{6,14},{7,63},{8,16},{9,1... | collective-permute-start | bytes 786440 | tf_op jit(solution)/shard_map/ppermute | solution.py:27
  15.4 6.7 %collective-permute-start.5 = (bf16[1024,128]{1,0:T(8,128)(2,1)S(1)}, bf16[1024,128]{1,0:T(8,128)(2,1)S(1)}, u32[]{:S(2)}, u32[]{:S(2)}) collective-permute-start(bf16[1024,128]{1,0:T(8,128)(2,1)S(1)} %collective-permute-done.2.refs_0_.refs_1_), channel_id=1, source_target_pairs={{0,8},{1,57},{2,10},{3,59},{4,12},{5,61},{6,14},{7,63},{8,16},{9,1... | collective-permute-start | bytes 786440 | tf_op jit(solution)/shard_map/ppermute | solution.py:27
  18.8 13.3 %collective-permute-start.4 = (bf16[2048,128]{1,0:T(8,128)(2,1)S(1)}, bf16[2048,128]{1,0:T(8,128)(2,1)S(1)}, u32[]{:S(2)}, u32[]{:S(2)}) collective-permute-start(bf16[2048,128]{1,0:T(8,128)(2,1)S(1)} %collective-permute-done.3.refs_2_), channel_id=1, source_target_pairs={{0,1},{1,0},{2,3},{3,2},{4,5},{5,4},{6,7},{7,6},{8,9},{9,8},{10,11... | collective-permute-start | bytes 1572872 | tf_op jit(solution)/shard_map/ppermute | solution.py:27
  22.2 7.2 %collective-permute-start.8 = (bf16[1024,128]{1,0:T(8,128)(2,1)S(1)}, bf16[1024,128]{1,0:T(8,128)(2,1)S(1)}, u32[]{:S(2)}, u32[]{:S(2)}) collective-permute-start(bf16[1024,128]{1,0:T(8,128)(2,1)S(1)} %collective-permute-done.5.refs_0_.refs_2_), channel_id=1, source_target_pairs={{0,8},{1,57},{2,10},{3,59},{4,12},{5,61},{6,14},{7,63},{8,16},{9,1... | collective-permute-start | bytes 786440 | tf_op jit(solution)/shard_map/ppermute | solution.py:27
  25.3 6.8 %collective-permute-start.6 = (bf16[1024,128]{1,0:T(8,128)(2,1)S(1)}, bf16[1024,128]{1,0:T(8,128)(2,1)S(1)}, u32[]{:S(2)}, u32[]{:S(2)}) collective-permute-start(bf16[1024,128]{1,0:T(8,128)(2,1)S(1)} %slice.8), channel_id=1, source_target_pairs={{0,2},{1,7},{2,4},{3,1},{4,6},{5,3},{6,0},{7,5},{8,10},{9,15},{10,... | collective-permute-start | bytes 786440 | tf_op jit(solution)/shard_map/ppermute | solution.py:27
  29.4 15.7 %collective-permute-start.9 = (bf16[512,128]{1,0:T(8,128)(2,1)S(1)}, bf16[512,128]{1,0:T(8,128)(2,1)S(1)}, u32[]{:S(2)}, u32[]{:S(2)}) collective-permute-start(bf16[512,128]{1,0:T(8,128)(2,1)S(1)} %slice.9), channel_id=1, source_target_pairs={{0,8},{1,57},{2,10},{3,59},{4,12},{5,61},{6,14},{7,63},{8,16},{9,1... | collective-permute-start | bytes 393224 | tf_op jit(solution)/shard_map/ppermute | solution.py:27
  32.1 3.5 %collective-permute-start.7 = (bf16[1024,128]{1,0:T(8,128)(2,1)S(1)}, bf16[1024,128]{1,0:T(8,128)(2,1)S(1)}, u32[]{:S(2)}, u32[]{:S(2)}) collective-permute-start(bf16[1024,128]{1,0:T(8,128)(2,1)S(1)} %collective-permute-done.6.refs_3_.refs_4_), channel_id=1, source_target_pairs={{0,1},{1,0},{2,3},{3,2},{4,5},{5,4},{6,7},{7,6},{8,9},{9,8},{10,11... | collective-permute-start | bytes 786440 | tf_op jit(solution)/shard_map/ppermute | solution.py:27

commit v2 on v1

v2 whole, which is shorter than its diff:
```python
import jax
import jax.numpy as jnp
from jax import lax
from jax.experimental import pallas as pl
from jax.experimental.pallas import tpu as pltpu
from jax.sharding import Mesh, PartitionSpec as P

BLOCK = 1024
AXES = ("x", "z", "y", "c")
SIZES = (4, 8, 4, 2)
LIMIT = 16 << 20
VMEM = pl.BlockSpec(memory_space=pltpu.VMEM)
KEPT = [(0, 0), (1, 0), (2, 0), (3, 0), (4, 0)]
SWAPPED = [(1, 1), (2, 1), (3, 1)]


def flat(x, z, y, c):
    return ((x * SIZES[1] + z) * SIZES[2] + y) * SIZES[3] + c


def move(value, target):
    pairs = []
    for x in range(SIZES[0]):
        for z in range(SIZES[1]):
            for y in range(SIZES[2]):
                for c in range(SIZES[3]):
                    pairs.append((flat(x, z, y, c), flat(*target(x, z, y, c))))
    return lax.ppermute(value, AXES, pairs)


def along(c):
    return 2 * c - 1


def to_partner(value):
    return move(value, lambda x, z, y, c: (x, z, y, 1 - c))


def down_z(value, steps=1):
    return move(value, lambda x, z, y, c: (x, (z - steps * along(c)) % SIZES[1], y, c))


def down_y(value, steps=1):
    return move(value, lambda x, z, y, c: (x, z, (y - steps * along(c)) % SIZES[2], c))


def after(value, *earlier):
    return lax.optimization_barrier((value, *earlier))[0]


def score_row(caps, items):
    best = None
    for at in range(0, BLOCK, 256):
        score = lax.dot_general(
            items[at : at + 256], caps, (((1,), (1,)), ((), ())),
            preferred_element_type=jnp.float32,
        )
        part = jnp.max(score.reshape(32, 8, 512), axis=0)
        best = part if best is None else jnp.maximum(best, part)
    return jnp.max(best, axis=0, keepdims=True)


def pieces(refs, height):
    return [r.at[at : at + height, :] for r in refs for at in range(0, r.shape[0], height)]


def scores(groups, blocks):
    n = len(groups)

    def body(*refs):
        out = refs[-1]
        items = pieces(refs[n:-1], BLOCK)
        for g, cref in enumerate(pieces(refs[:n], 512)):
            own = cref[...]
            for b, iref in enumerate(items):
                out[pl.ds(g * len(items) + b, 1), :] = score_row(own, iref)

    rows = sum(v.shape[0] // 512 for v in groups) * sum(v.shape[0] // BLOCK for v in blocks)
    return pl.pallas_call(
        body,
        out_shape=jax.ShapeDtypeStruct((rows, 512), jnp.float32),
        in_specs=[VMEM] * (n + len(blocks)),
        out_specs=VMEM,
        compiler_params=pltpu.CompilerParams(vmem_limit_bytes=LIMIT),
        cost_estimate=pl.CostEstimate(
            flops=rows * 2 * 512 * BLOCK * 128 * 2, bytes_accessed=1 << 16, transcendentals=0
        ),
    )(*groups, *blocks)


def user_rows(parts, groups):
    n = len(groups)
    used = [(v, names) for v, names in parts if any(name and name[0] in groups for name in names)]

    def body(*refs):
        out, rows = refs[-2], refs[-1]
        y = lax.axis_index("y")
        c = lax.axis_index("c")
        for ref, (_, names) in zip(refs, used):
            for r, (group, (dy, other)) in enumerate(names):
                if group in groups:
                    at = ((y + along(c) * dy + 4) % 4) * 2 + (1 - c if other else c)
                    place = (at // 4) * (4 * n) + groups.index(group) * 4 + at % 4
                    rows[pl.ds(place, 1), :] = ref[r : r + 1, :]
        by_user = jnp.max(rows[...].T.reshape(64, 8, 8 * n), axis=1)
        halves = jnp.concatenate([by_user[:, : 4 * n], by_user[:, 4 * n :]], axis=0)
        out[...] = halves.T.reshape(n, 4, 128)

    return pl.pallas_call(
        body,
        out_shape=jax.ShapeDtypeStruct((n, 4, 128), jnp.float32),
        in_specs=[VMEM] * len(used),
        out_specs=VMEM,
        compiler_params=pltpu.CompilerParams(vmem_limit_bytes=LIMIT),
        scratch_shapes=[pltpu.VMEM((8 * n, 512), jnp.float32)],
    )(*[v for v, _ in used])


def by_owner(kept, swapped):
    def body(kept_ref, swapped_ref, out):
        z = lax.axis_index("z")
        step = along(lax.axis_index("c"))
        for x in range(SIZES[0]):
            for i, (dz, _) in enumerate(KEPT):
                out[x * 8 + (z + step * dz + 8) % 8] = kept_ref[i]
            for i, (dz, _) in enumerate(SWAPPED):
                out[x * 8 + (z - step * dz + 8) % 8] = swapped_ref[i]

    return pl.pallas_call(
        body,
        out_shape=jax.ShapeDtypeStruct((32, 4, 128), jnp.float32),
        in_specs=[VMEM, VMEM],
        out_specs=VMEM,
        compiler_params=pltpu.CompilerParams(vmem_limit_bytes=LIMIT),
    )(kept, swapped)


def finish(table):
    def body(table_ref, relative, peak):
        x = lax.axis_index("x")
        top = jnp.max(jnp.max(table_ref[...], axis=0), axis=0, keepdims=True)
        top = jnp.maximum(top[:, :64], top[:, 64:])
        mine = [table_ref[x * 8 + z] for z in range(8)]
        rows = jnp.concatenate([part for m in mine for part in (m[:, :64], m[:, 64:])], axis=0)
        relative[...] = (rows - top).T
        peak[...] = top[0]

    return pl.pallas_call(
        body,
        out_shape=(jax.ShapeDtypeStruct((64, 64), jnp.float32), jax.ShapeDtypeStruct((64,), jnp.float32)),
        in_specs=[VMEM],
        out_specs=(VMEM, VMEM),
        compiler_params=pltpu.CompilerParams(vmem_limit_bytes=LIMIT),
    )(table)


def peaks(capsules, bank):
    own = capsules.reshape(512, 128)
    own_x = to_partner(own)
    bank_x = to_partner(bank)
    own_pair = jnp.concatenate([own, own_x], axis=0)
    block_pair = jnp.concatenate([bank, bank_x], axis=0)
    here, ahead, behind, far, far_x = [(0, 0), (0, 1)], [(1, 0), (1, 1)], [(-1, 1), (-1, 0)], [(2, 0)], [(2, 1)]
    g0, g1, g2, g3, g4 = [(0, 0)], [(1, 0), (1, 1)], [(2, 0), (2, 1)], [(3, 0), (3, 1)], [(4, 0)]
    parts = []

    def score(caps, groups, items, blocks):
        parts.append((scores(caps, items), [(g, b) for g in groups for b in blocks]))

    z1 = down_z(own_pair)
    y1 = down_y(block_pair)
    z2 = down_z(own_pair, 2)
    y2 = down_y(y1[:BLOCK])
    z3 = down_z(z1, 2)
    y1x = to_partner(y1)
    y2x = to_partner(y2)
    score([own], g0, [block_pair], here)
    score([z1], g1, [block_pair], here)
    score([own, z1], g0 + g1, [y1], ahead)
    score([own, z1], g0 + g1, [y1x], behind)
    score([z2], g2, [block_pair, y1, y1x], here + ahead + behind)
    far_half = after(z3, parts[-1][0])[:512]
    z4 = down_z(far_half)
    score([z3], g3, [block_pair, y1, y1x], here + ahead + behind)
    score([own, z1, z2, z3], g0 + g1 + g2 + g3, [y2, y2x], far + far_x)
    rows = user_rows(parts, SWAPPED)
    swapped = to_partner(rows)
    score([z4], g4, [block_pair, y1, y1x, y2, y2x], here + ahead + behind + far + far_x)
    table = lax.all_to_all(by_owner(user_rows(parts, KEPT), swapped), ("x", "z"), 0, 0, tiled=True)
    return finish(table)


def solution(mesh):
    grid = Mesh(mesh.devices.reshape(SIZES), AXES)
    return jax.shard_map(
        peaks,
        mesh=grid,
        in_specs=(P(("z", "y", "c"), None, None), P(AXES, None)),
        out_specs=(P(("z", "y", "c"), "x"), P(("z", "y", "c"))),
        check_vma=False,
    )
```

time: 69.2 us -> 67.7 us (0.978)
  blocking collectives: 20.4 us -> 14.8 us
  waiting for transfers between devices: 6.94 us -> 11.8 us
  starting transfers between devices: 19.6 us -> 18.7 us
    all_to_all x1, blocking collectives: 20.4 us -> 14.8 us  [peaks(): lax.all_to_all(by_owner(user_rows(parts, KEPT), swapped), ('x', 'z'), 0,...]
    ppermute x10 -> x11, waiting for transfers between devices: 6.94 us -> 11.8 us  [move(): return lax.ppermute(value, AXES, pairs)]
    ppermute x10 -> x11, starting transfers between devices: 19.6 us -> 18.7 us  [move(): return lax.ppermute(value, AXES, pairs)]
  transfers between devices with their start and end apart: 10 -> 11, of which waited for: 3 -> 4; matrix products, arithmetic and copies ran while one was open for 2% -> 1% of each run, Pallas kernels for 24% -> 29%
where the time goes in v2:
time: 67.7 us; the launch traced here: 67.6 us
  Pallas kernels  20.4 us (30%)
  starting transfers between devices  18.7 us (28%)
  blocking collectives  14.8 us (22%)
  waiting for transfers between devices  11.8 us (17%)
  local copies, waits for them, and re-layouts  1.04 us (2%)
  between operations  0.78 us (1%)
    pallas_call x8, Pallas kernels, scores(): pl.pallas_call(body, out_shape=jax.ShapeDtypeStruct((rows, 512), jnp.floa...  18.9 us
    ppermute x11, starting transfers between devices, move(): return lax.ppermute(value, AXES, pairs)  18.7 us
    all_to_all x1, blocking collectives, peaks(): lax.all_to_all(by_owner(user_rows(parts, KEPT), swapped), ('x', 'z'), 0,...  14.8 us
    ppermute x11, waiting for transfers between devices, move(): return lax.ppermute(value, AXES, pairs)  11.8 us
  transfers between devices with their start and end apart: 11, of which 4 were waited for; matrix products, arithmetic and copies ran while one was open for 1% of the time, Pallas kernels for 29%

profile of v2, /device:TPU:1, one launch (start us, length us, event | category | flops | bytes accessed | tf_op | source)
XLA Modules:
  0.0 67.6 jit_solution(12560399335466964628)
XLA Ops:
  0.6 3.3 %collective-permute-start = (bf16[1024,128]{1,0:T(8,128)(2,1)}, bf16[1024,128]{1,0:T(8,128)(2,1)S(1)}, u32[]{:S(2)}, u32[]{:S(2)}) collective-permute-start(bf16[1024,128]{1,0:T(8,128)(2,1)} %param.3), channel_id=1, source_target_pairs={{0,1},{1,0},{2,3},{3,2},{4,5},{5,4},{6,7},{7,6},{8,9},{9,8},{10,11... | collective-permute-start | bytes 786440 | tf_op jit(solution)/shard_map/ppermute | solution.py:28
  3.9 1.0 %constant_dynamic-update-slice_fusion.1 = bf16[2048,128]{1,0:T(8,128)(2,1)S(1)} fusion(bf16[1024,128]{1,0:T(8,128)(2,1)} %param.3), kind=kLoop, calls=%fused_computation.2 | loop fusion | bytes 524288
  4.9 0.0 copy-start
  4.9 0.4 collective-permute-done
  5.3 1.1 %collective-permute-start.3 = (bf16[2048,128]{1,0:T(8,128)(2,1)S(1)}, bf16[2048,128]{1,0:T(8,128)(2,1)S(1)}, u32[]{:S(2)}, u32[]{:S(2)}) collective-permute-start(bf16[2048,128]{1,0:T(8,128)(2,1)S(1)} %constant_dynamic-update-slice_fusion.refs_1_), channel_id=1, source_target_pairs={{0,2},{1,7},{2,4},{3,1},{4,6},{5,3},{6,0},{7,5},{8,10},{9,15},{10,... | collective-permute-start | bytes 1572872 | tf_op jit(solution)/shard_map/ppermute | solution.py:28
  6.4 0.0 collective-permute-start.1
  6.4 7.3 %collective-permute-done.3.refs_2_ = bf16[2048,128]{1,0:T(8,128)(2,1)S(1)} collective-permute-done((bf16[2048,128]{1,0:T(8,128)(2,1)S(1)}, bf16[2048,128]{1,0:T(8,128)(2,1)S(1)}, u32[]{:S(2)}, u32[]{:S(2)}) %collective-permute-start.3) | collective-permute-done | bytes 524320 | tf_op jit(solution)/shard_map/ppermute | solution.py:28
  13.7 2.4 %collective-permute-start.4 = (bf16[2048,128]{1,0:T(8,128)(2,1)S(1)}, bf16[2048,128]{1,0:T(8,128)(2,1)S(1)}, u32[]{:S(2)}, u32[]{:S(2)}) collective-permute-start(bf16[2048,128]{1,0:T(8,128)(2,1)S(1)} %collective-permute-done.3.refs_2_), channel_id=1, source_target_pairs={{0,1},{1,0},{2,3},{3,2},{4,5},{5,4},{6,7},{7,6},{8,9},{9,8},{10,11... | collective-permute-start | bytes 1572872 | tf_op jit(solution)/shard_map/ppermute | solution.py:28
  16.2 0.0 collective-permute-done.1
  16.2 3.9 %collective-permute-start.2 = (bf16[1024,128]{1,0:T(8,128)(2,1)S(1)}, bf16[1024,128]{1,0:T(8,128)(2,1)S(1)}, u32[]{:S(2)}, u32[]{:S(2)}) collective-permute-start(bf16[1024,128]{1,0:T(8,128)(2,1)S(1)} %pad_maximum_fusion), channel_id=1, source_target_pairs={{0,8},{1,57},{2,10},{3,59},{4,12},{5,61},{6,14},{7,63},{8,16},{9,1... | collective-permute-start | bytes 786440 | tf_op jit(solution)/shard_map/ppermute | solution.py:28
  20.1 1.2 %collective-permute-start.5 = (bf16[1024,128]{1,0:T(8,128)(2,1)S(1)}, bf16[1024,128]{1,0:T(8,128)(2,1)S(1)}, u32[]{:S(2)}, u32[]{:S(2)}) collective-permute-start(bf16[1024,128]{1,0:T(8,128)(2,1)S(1)} %pad_maximum_fusion), channel_id=1, source_target_pairs={{0,16},{1,49},{2,18},{3,51},{4,20},{5,53},{6,22},{7,55},{8,24},{9,... | collective-permute-start | bytes 786440 | tf_op jit(solution)/shard_map/ppermute | solution.py:28
  21.3 1.6 %collective-permute-start.7 = (bf16[1024,128]{1,0:T(8,128)(2,1)S(1)}, bf16[1024,128]{1,0:T(8,128)(2,1)S(1)}, u32[]{:S(2)}, u32[]{:S(2)}) collective-permute-start(bf16[1024,128]{1,0:T(8,128)(2,1)S(1)} %slice.8), channel_id=1, source_target_pairs={{0,2},{1,7},{2,4},{3,1},{4,6},{5,3},{6,0},{7,5},{8,10},{9,15},{10,... | collective-permute-start | bytes 786440 | tf_op jit(solution)/shard_map/ppermute | solution.py:28
  22.9 0.7 %shard_map.41.refs_0_ = f32[2,512]{1,0:T(2,128)S(1)} custom-call(bf16[512,128]{1,0:T(8,128)(2,1)S(1)} %bitcast.3, bf16[2048,128]{1,0:T(8,128)(2,1)S(1)} %constant_dynamic-update-slice_fusion.refs_1_), custom_call_target="tpu_custom_call" | custom-call | flops 536870912 | bytes 65536 | tf_op jit(solution)/shard_map/pallas_call | solution.py:79
  23.7 2.2 %collective-permute-done.2.refs_0_.refs_1_ = bf16[1024,128]{1,0:T(8,128)(2,1)S(1)} collective-permute-done((bf16[1024,128]{1,0:T(8,128)(2,1)S(1)}, bf16[1024,128]{1,0:T(8,128)(2,1)S(1)}, u32[]{:S(2)}, u32[]{:S(2)}) %collective-permute-start.2) | collective-permute-done | bytes 262176 | tf_op jit(solution)/shard_map/ppermute | solution.py:28
  25.9 0.2 collective-permute-start.6
  26.1 1.3 %shard_map.42.refs_1_.refs_0_ = f32[4,512]{1,0:T(4,128)S(1)} custom-call(bf16[1024,128]{1,0:T(8,128)(2,1)S(1)} %collective-permute-done.2.refs_0_.refs_1_, bf16[2048,128]{1,0:T(8,128)(2,1)S(1)} %constant_dynamic-update-slice_fusion.refs_1_), custom_call_target="tpu_custom_call" | custom-call | flops 1073741824 | bytes 65536 | tf_op jit(solution)/shard_map/pallas_call | solution.py:79
  27.4 1.8 %shard_map.43.refs_2_.refs_1_ = f32[6,512]{1,0:T(8,128)S(1)} custom-call(bf16[512,128]{1,0:T(8,128)(2,1)S(1)} %bitcast.4, bf16[1024,128]{1,0:T(8,128)(2,1)S(1)} %collective-permute-done.2.refs_0_.refs_1_, bf16[2048,128]{1,0:T(8,128)(2,1)S(1)} %collective-permute-done.3.refs_2_), custom_call_target="tpu_custom_call" | custom-call | flops 1610612736 | bytes 65536 | tf_op jit(solution)/shard_map/pallas_call | solution.py:79
  29.2 0.0 collective-permute-done.7.refs_4_
  29.2 0.3 collective-permute-start.8
  29.5 1.9 %collective-permute-done.5.refs_0_.refs_2_ = bf16[1024,128]{1,0:T(8,128)(2,1)S(1)} collective-permute-done((bf16[1024,128]{1,0:T(8,128)(2,1)S(1)}, bf16[1024,128]{1,0:T(8,128)(2,1)S(1)}, u32[]{:S(2)}, u32[]{:S(2)}) %collective-permute-start.5) | collective-permute-done | bytes 262176 | tf_op jit(solution)/shard_map/ppermute | solution.py:28
  31.4 3.5 %shard_map.45.refs_4_.refs_3_ = f32[12,512]{1,0:T(8,128)S(1)} custom-call(bf16[1024,128]{1,0:T(8,128)(2,1)S(1)} %collective-permute-done.5.refs_0_.refs_2_, bf16[2048,128]{1,0:T(8,128)(2,1)S(1)} %constant_dynamic-update-slice_fusion.refs_1_, bf16[2048,128]{1,0:T(8,128)(2,1)S(1)} %collective-permute-done.3.refs_2_, ...), custom_call_target="tpu_custom_call" | custom-call | flops 3221225472 | bytes 65536 | tf_op jit(solution)/shard_map/pallas_call | solution.py:79
  34.9 4.3 %collective-permute-start.9 = (bf16[512,128]{1,0:T(8,128)(2,1)S(1)}, bf16[512,128]{1,0:T(8,128)(2,1)S(1)}, u32[]{:S(2)}, u32[]{:S(2)}) collective-permute-start(bf16[512,128]{1,0:T(8,128)(2,1)S(1)} %slice.7), channel_id=1, source_target_pairs={{0,8},{1,57},{2,10},{3,59},{4,12},{5,61},{6,14},{7,63},{8,16},{9,1... | collective-permute-start | bytes 393224 | tf_op jit(solution)/shard_map/ppermute | solution.py:28
  39.2 3.5 %shard_map.46.refs_5_.refs_4_ = f32[12,512]{1,0:T(8,128)S(1)} custom-call(bf16[1024,128]{1,0:T(8,128)(2,1)S(1)} %collective-permute-done.6.refs_0_.refs_3_, bf16[2048,128]{1,0:T(8,128)(2,1)S(1)} %constant_dynamic-update-slice_fusion.refs_1_, bf16[2048,128]{1,0:T(8,128)(2,1)S(1)} %collective-permute-done.3.refs_2_, ...), custom_call_target="tpu_custom_call" | custom-call | flops 3221225472 | bytes 65536 | tf_op jit(solution)/shard_map/pallas_call | solution.py:79
  42.7 4.0 %shard_map.47.refs_6_.refs_5_ = f32[14,512]{1,0:T(8,128)S(1)} custom-call(bf16[512,128]{1,0:T(8,128)(2,1)S(1)} %bitcast.5, bf16[1024,128]{1,0:T(8,128)(2,1)S(1)} %collective-permute-done.2.refs_0_.refs_1_, bf16[1024,128]{1,0:T(8,128)(2,1)S(1)} %collective-permute-done.5.refs_0_.refs_2_, bf16[1024,128]{1,0:T(8,128)(2,1)S(1)} %collective-permute-done.6.refs_0_.refs_3_, ...), custom_call_target="tpu_custom_call" | custom-call | flops 3758096384 | bytes 65536 | tf_op jit(solution)/shard_map/pallas_call | solution.py:79
  46.7 1.8 %shard_map.44.refs_3_.refs_2_ = f32[6,512]{1,0:T(8,128)S(1)} custom-call(bf16[512,128]{1,0:T(8,128)(2,1)S(1)} %bitcast.6, bf16[1024,128]{1,0:T(8,128)(2,1)S(1)} %collective-permute-done.2.refs_0_.refs_1_, bf16[2048,128]{1,0:T(8,128)(2,1)S(1)} %collective-permute-done.4.refs_2_.refs_3_), custom_call_target="tpu_custom_call" | custom-call | flops 1610612736 | bytes 65536 | tf_op jit(solution)/shard_map/pallas_call | solution.py:79
  48.5 0.3 shard_map.50
  48.8 0.3 collective-permute-start.10
  49.1 2.4 %shard_map.48.refs_7_ = f32[8,512]{1,0:T(8,128)S(1)} custom-call(bf16[512,128]{1,0:T(8,128)(2,1)S(1)} %collective-permute-done.9.refs_0_, bf16[2048,128]{1,0:T(8,128)(2,1)S(1)} %constant_dynamic-update-slice_fusion.refs_1_, bf16[2048,128]{1,0:T(8,128)(2,1)S(1)} %collective-permute-done.3.refs_2_, ...), custom_call_target="tpu_custom_call" | custom-call | flops 2147483648 | bytes 65536 | tf_op jit(solution)/shard_map/pallas_call | solution.py:79
  51.5 0.4 shard_map.49.kept_ref
  51.9 0.1 shard_map.51
  52.0 14.8 %all_to_all.5.table_ref = f32[32,4,128]{2,1,0:T(4,128)S(1)} all-to-all(f32[32,4,128]{2,1,0:T(4,128)S(1)} %shard_map.51), channel_id=1, replica_groups=mesh['x'=4,'z'=8,'y'=4,'c'=2] {'x','z'}, dimensions={0} | all-to-all | bytes 131072 | tf_op jit(solution)/shard_map/all_to_all | solution.py:189
  66.8 0.8 %shard_map.52 = (f32[64,64]{1,0:T(8,128)}, f32[64]{0:T(128)}) custom-call(f32[32,4,128]{2,1,0:T(4,128)S(1)} %all_to_all.5.table_ref), custom_call_target="tpu_custom_call" | custom-call | tf_op jit(solution)/shard_map/pallas_call | solution.py:148
  (10 shorter events, 0.1 us)
Async XLA Ops:
  0.6 4.7 %collective-permute-start = (bf16[1024,128]{1,0:T(8,128)(2,1)}, bf16[1024,128]{1,0:T(8,128)(2,1)S(1)}, u32[]{:S(2)}, u32[]{:S(2)}) collective-permute-start(bf16[1024,128]{1,0:T(8,128)(2,1)} %param.3), channel_id=1, source_target_pairs={{0,1},{1,0},{2,3},{3,2},{4,5},{5,4},{6,7},{7,6},{8,9},{9,8},{10,11... | collective-permute-start | bytes 786440 | tf_op jit(solution)/shard_map/ppermute | solution.py:28
  4.9 1.5 %copy-start = (bf16[64,8,128]{2,1,0:T(8,128)(2,1)S(1)}, bf16[64,8,128]{2,1,0:T(8,128)(2,1)}, u32[]{:S(2)}) copy-start(bf16[64,8,128]{2,1,0:T(8,128)(2,1)} %param.2) | copy-start | bytes 393220
  5.3 8.4 %collective-permute-start.3 = (bf16[2048,128]{1,0:T(8,128)(2,1)S(1)}, bf16[2048,128]{1,0:T(8,128)(2,1)S(1)}, u32[]{:S(2)}, u32[]{:S(2)}) collective-permute-start(bf16[2048,128]{1,0:T(8,128)(2,1)S(1)} %constant_dynamic-update-slice_fusion.refs_1_), channel_id=1, source_target_pairs={{0,2},{1,7},{2,4},{3,1},{4,6},{5,3},{6,0},{7,5},{8,10},{9,15},{10,... | collective-permute-start | bytes 1572872 | tf_op jit(solution)/shard_map/ppermute | solution.py:28
  6.4 9.7 %collective-permute-start.1 = (bf16[512,128]{1,0:T(8,128)(2,1)S(1)}, bf16[512,128]{1,0:T(8,128)(2,1)S(1)}, u32[]{:S(2)}, u32[]{:S(2)}) collective-permute-start(bf16[512,128]{1,0:T(8,128)(2,1)S(1)} %bitcast.1), channel_id=1, source_target_pairs={{0,1},{1,0},{2,3},{3,2},{4,5},{5,4},{6,7},{7,6},{8,9},{9,8},{10,11... | collective-permute-start | bytes 393224 | tf_op jit(solution)/shard_map/ppermute | solution.py:28
  13.7 17.7 %collective-permute-start.4 = (bf16[2048,128]{1,0:T(8,128)(2,1)S(1)}, bf16[2048,128]{1,0:T(8,128)(2,1)S(1)}, u32[]{:S(2)}, u32[]{:S(2)}) collective-permute-start(bf16[2048,128]{1,0:T(8,128)(2,1)S(1)} %collective-permute-done.3.refs_2_), channel_id=1, source_target_pairs={{0,1},{1,0},{2,3},{3,2},{4,5},{5,4},{6,7},{7,6},{8,9},{9,8},{10,11... | collective-permute-start | bytes 1572872 | tf_op jit(solution)/shard_map/ppermute | solution.py:28
  16.2 9.7 %collective-permute-start.2 = (bf16[1024,128]{1,0:T(8,128)(2,1)S(1)}, bf16[1024,128]{1,0:T(8,128)(2,1)S(1)}, u32[]{:S(2)}, u32[]{:S(2)}) collective-permute-start(bf16[1024,128]{1,0:T(8,128)(2,1)S(1)} %pad_maximum_fusion), channel_id=1, source_target_pairs={{0,8},{1,57},{2,10},{3,59},{4,12},{5,61},{6,14},{7,63},{8,16},{9,1... | collective-permute-start | bytes 786440 | tf_op jit(solution)/shard_map/ppermute | solution.py:28
  20.1 11.3 %collective-permute-start.5 = (bf16[1024,128]{1,0:T(8,128)(2,1)S(1)}, bf16[1024,128]{1,0:T(8,128)(2,1)S(1)}, u32[]{:S(2)}, u32[]{:S(2)}) collective-permute-start(bf16[1024,128]{1,0:T(8,128)(2,1)S(1)} %pad_maximum_fusion), channel_id=1, source_target_pairs={{0,16},{1,49},{2,18},{3,51},{4,20},{5,53},{6,22},{7,55},{8,24},{9,... | collective-permute-start | bytes 786440 | tf_op jit(solution)/shard_map/ppermute | solution.py:28
  21.3 7.9 %collective-permute-start.7 = (bf16[1024,128]{1,0:T(8,128)(2,1)S(1)}, bf16[1024,128]{1,0:T(8,128)(2,1)S(1)}, u32[]{:S(2)}, u32[]{:S(2)}) collective-permute-start(bf16[1024,128]{1,0:T(8,128)(2,1)S(1)} %slice.8), channel_id=1, source_target_pairs={{0,2},{1,7},{2,4},{3,1},{4,6},{5,3},{6,0},{7,5},{8,10},{9,15},{10,... | collective-permute-start | bytes 786440 | tf_op jit(solution)/shard_map/ppermute | solution.py:28
  25.9 9.0 %collective-permute-start.6 = (bf16[1024,128]{1,0:T(8,128)(2,1)S(1)}, bf16[1024,128]{1,0:T(8,128)(2,1)S(1)}, u32[]{:S(2)}, u32[]{:S(2)}) collective-permute-start(bf16[1024,128]{1,0:T(8,128)(2,1)S(1)} %collective-permute-done.2.refs_0_.refs_1_), channel_id=1, source_target_pairs={{0,16},{1,49},{2,18},{3,51},{4,20},{5,53},{6,22},{7,55},{8,24},{9,... | collective-permute-start | bytes 786440 | tf_op jit(solution)/shard_map/ppermute | solution.py:28
  29.2 13.5 %collective-permute-start.8 = (bf16[1024,128]{1,0:T(8,128)(2,1)S(1)}, bf16[1024,128]{1,0:T(8,128)(2,1)S(1)}, u32[]{:S(2)}, u32[]{:S(2)}) collective-permute-start(bf16[1024,128]{1,0:T(8,128)(2,1)S(1)} %collective-permute-done.7.refs_4_), channel_id=1, source_target_pairs={{0,1},{1,0},{2,3},{3,2},{4,5},{5,4},{6,7},{7,6},{8,9},{9,8},{10,11... | collective-permute-start | bytes 786440 | tf_op jit(solution)/shard_map/ppermute | solution.py:28
  34.9 14.2 %collective-permute-start.9 = (bf16[512,128]{1,0:T(8,128)(2,1)S(1)}, bf16[512,128]{1,0:T(8,128)(2,1)S(1)}, u32[]{:S(2)}, u32[]{:S(2)}) collective-permute-start(bf16[512,128]{1,0:T(8,128)(2,1)S(1)} %slice.7), channel_id=1, source_target_pairs={{0,8},{1,57},{2,10},{3,59},{4,12},{5,61},{6,14},{7,63},{8,16},{9,1... | collective-permute-start | bytes 393224 | tf_op jit(solution)/shard_map/ppermute | solution.py:28
  48.8 3.0 %collective-permute-start.10 = (f32[3,4,128]{2,1,0:T(4,128)S(1)}, f32[3,4,128]{2,1,0:T(4,128)S(1)}, u32[]{:S(2)}, u32[]{:S(2)}) collective-permute-start(f32[3,4,128]{2,1,0:T(4,128)S(1)} %shard_map.50), channel_id=1, source_target_pairs={{0,1},{1,0},{2,3},{3,2},{4,5},{5,4},{6,7},{7,6},{8,9},{9,8},{10,11... | collective-permute-start | bytes 18440 | tf_op jit(solution)/shard_map/ppermute | solution.py:28
